TPU v7x, 32 devices: a whole 2x2x4 slice. The times are simulated.
32 devices in a mesh: grp: 2 (over y), page: 16 (over z, x, core).
Axes of the slice: x: 2, y: 2, z: 4, core: 2. Of those that a mesh axis runs over, the one named last changes fastest.
Arguments:
- queries: bfloat16 [32, 4096], P('grp'), parts along dimension 0, may hold values from -64 to 64
- key_cache: bfloat16 [1024, 64, 1024], P(('grp', 'page')), parts along dimension 0, may hold values from -9 to 9
- value_cache: bfloat16 [1024, 64, 1024], P(('grp', 'page')), parts along dimension 0, may hold values from -16 to 16
- new_keys: bfloat16 [32, 1024], P('grp'), parts along dimension 0, may hold values from -16 to 16
- new_values: bfloat16 [32, 1024], P('grp'), parts along dimension 0, may hold values from -6 to 6
- chosen: int32 [16, 256], P('grp', 'page'), parts along dimension 0, may hold values from 0 to 511, as said below
Outputs:
- attended: bfloat16 [32, 4096], P('grp'), parts along dimension 0
There are 2 independent parts, one for each index of `grp`. A program takes and returns all parts, laid end to end along the dimension named above; each array names one. Nothing has to cross between parts.
Inputs may be any that keep to these rules, and one draw needn't show every extreme that they name: `chosen`: each row names 256 different pages; at most 32 of a row's pages lie in the range of 32 pages of one device, and exactly 32 do for some device in every row.
All inputs are finite; a program needn't handle non-finite values.
Results may differ from a plain program's by a relative error of at most 0.004.
Values may be sent and summed in bfloat16 or wider, within the bound.
A program may use at most 64 MiB of HBM per device.

v0:
```python
import jax
import jax.numpy as jnp
from jax import lax
from jax.sharding import PartitionSpec as P

FLOOR_SCORE = -1e30


def combine(former, latter):
    high_a, sums_a, weighted_a = former
    high_b, sums_b, weighted_b = latter
    highest = jnp.maximum(high_a, high_b)
    factor_a = jnp.exp(high_a - highest)
    factor_b = jnp.exp(high_b - highest)
    return (
        highest,
        sums_a * factor_a + sums_b * factor_b,
        weighted_a * factor_a[..., None] + weighted_b * factor_b[..., None],
    )


def fresh_term(query_rows, key_rows, value_rows, depth_pos, scaling):
    scores = (
        jnp.einsum("nd,ntd->nt", query_rows, key_rows, preferred_element_type=jnp.float32) * scaling
    )
    allowed = jnp.arange(key_rows.shape[1], dtype=jnp.int32)[None, :] <= depth_pos[:, None]
    highest = jnp.max(jnp.where(allowed, scores, FLOOR_SCORE), axis=1)
    weights = jnp.where(allowed, jnp.exp(scores - highest[:, None]), 0.0).astype(jnp.bfloat16)
    totals = jnp.sum(weights.astype(jnp.float32), axis=1)
    weighted = jnp.einsum("nt,ntd->nd", weights, value_rows, preferred_element_type=jnp.float32)
    return (highest, totals, weighted)


def on_device(queries, key_cache, value_cache, new_keys, new_values, chosen):
    page_count, page_tokens, head_span = key_cache.shape
    chosen_all = lax.all_gather(chosen, "page", axis=1, tiled=True)
    kv_heads = chosen_all.shape[0]
    head_width = head_span // kv_heads
    drafts = queries.shape[0]
    groups = queries.shape[1] // head_span
    row_count = drafts * groups
    scaling = head_width ** (-0.5)
    query_heads = (
        queries.reshape(drafts, kv_heads, groups, head_width)
        .transpose(1, 0, 2, 3)
        .reshape(kv_heads, row_count, head_width)
    )
    local_pages = chosen_all - lax.axis_index("page") * page_count
    page_slots = jnp.arange(page_count, dtype=jnp.int32)
    picked = jnp.any(local_pages[:, :, None] == page_slots[None, None, :], axis=1)
    key_flat = key_cache.reshape(page_count * page_tokens, kv_heads, head_width)
    value_flat = value_cache.reshape(page_count * page_tokens, kv_heads, head_width)
    usable = jnp.repeat(picked, page_tokens, axis=1)
    scores = (
        jnp.einsum("hrd,nhd->hrn", query_heads, key_flat, preferred_element_type=jnp.float32)
        * scaling
    )
    scores = jnp.where(usable[:, None, :], scores, FLOOR_SCORE)
    highest = jnp.max(scores, axis=2)
    present = highest > 0.5 * FLOOR_SCORE
    offset = jnp.where(present, highest, 0.0)
    weights = jnp.where(usable[:, None, :], jnp.exp(scores - offset[..., None]), 0.0).astype(
        jnp.bfloat16
    )
    totals = jnp.sum(weights.astype(jnp.float32), axis=2)
    weighted = jnp.einsum("hrn,nhd->hrd", weights, value_flat, preferred_element_type=jnp.float32)
    all_rows = kv_heads * row_count
    highest = highest.reshape(all_rows)
    totals = totals.reshape(all_rows)
    weighted = weighted.reshape(all_rows, head_width)
    key_heads = new_keys.reshape(drafts, kv_heads, head_width).transpose(1, 0, 2)
    value_heads = new_values.reshape(drafts, kv_heads, head_width).transpose(1, 0, 2)
    query_flat = query_heads.reshape(all_rows, head_width)
    devices = lax.axis_size("page")
    share_rows = all_rows // devices
    pieces = (
        highest.reshape(devices, share_rows),
        totals.reshape(devices, share_rows),
        weighted.reshape(devices, share_rows, head_width),
    )
    high_in, sums_in, weighted_in = (
        lax.all_to_all(pieces[0], "page", split_axis=0, concat_axis=0, tiled=True),
        lax.all_to_all(pieces[1], "page", split_axis=0, concat_axis=0, tiled=True),
        lax.all_to_all(pieces[2], "page", split_axis=0, concat_axis=0, tiled=True),
    )
    merged_high = jnp.max(high_in, axis=0)
    factors = jnp.exp(high_in - merged_high[None, :])
    merged = (
        merged_high,
        jnp.sum(sums_in * factors, axis=0),
        jnp.sum(weighted_in * factors[..., None], axis=0),
    )
    first_row = lax.axis_index("page") * share_rows
    row_ids = first_row + jnp.arange(share_rows, dtype=jnp.int32)
    query_own = lax.dynamic_slice_in_dim(query_flat, first_row, share_rows, 0)
    head_ids = row_ids // row_count
    depth_pos = row_ids % row_count // groups
    fresh = fresh_term(query_own, key_heads[head_ids], value_heads[head_ids], depth_pos, scaling)
    final_high, final_sums, final_weighted = combine(merged, fresh)
    finished = (final_weighted / final_sums[:, None]).astype(jnp.bfloat16)
    result = lax.all_gather(finished, "page", axis=0, tiled=True)
    return (
        result.reshape(kv_heads, drafts, groups, head_width)
        .transpose(1, 0, 2, 3)
        .reshape(drafts, kv_heads * groups * head_width)
    )


def solution(mesh):
    placed = (
        P("grp", None),
        P(("grp", "page"), None, None),
        P(("grp", "page"), None, None),
        P("grp", None),
        P("grp", None),
        P("grp", "page"),
    )
    return jax.shard_map(
        on_device, mesh=mesh, in_specs=placed, out_specs=P("grp", None), check_vma=False
    )
```

profile of v0, /device:TPU:0, one launch (start us, length us, event | category | flops | bytes accessed | tf_op | source)
XLA Modules:
  0.0 91.0 jit_solution(6589487834992607965)
XLA Ops:
  0.0 0.0 copy-start
  0.0 1.0 %reshape.167 = bf16[16,8,4,128]{3,2,1,0:T(4,128)(2,1)S(1)} reshape(bf16[16,4096]{1,0:T(8,128)(2,1)} %param.6) | data formatting | bytes 262144 | tf_op jit(solution)/shard_map/reshape | solution.py:44
  1.0 23.5 %all-gather = s32[16,16,8]{1,2,0:T(8,128)S(1)} all-gather(s32[1,16,8]{1,2,0:T(8,128)} %bitcast.70), channel_id=1, replica_groups=mesh['grp'=2,'page'=16] {'page'}, dimensions={0}, use_global_device_ids=true | all-gather | bytes 8704 | tf_op jit(solution)/shard_map/all_gather | solution.py:36
  24.6 0.1 reshape.194
  24.7 0.2 fusion.5
  24.9 0.1 broadcast_in_dim.47
  25.0 0.1 broadcast_in_dim.48
  25.1 3.3 %copy.42 = bf16[256,8,8,128]{3,2,1,0:T(8,128)(2,1)S(1)} copy(bf16[256,8,8,128]{3,1,2,0:T(8,128)(2,1)} %bitcast.60) | data formatting | bytes 8388608
  28.4 1.7 %fusion.4 = (f32[8,64]{1,0:T(8,128)S(1)}, f32[8,64,2048]{2,1,0:T(8,128)S(1)}) fusion(pred[8,2048]{1,0:T(8,128)(4,1)S(1)} %broadcast_in_dim.48, bf16[8,64,128]{2,1,0:T(8,128)(2,1)S(1)} %bitcast.63, bf16[2048,8,128]{2,1,0:T(8,128)(2,1)S(1)} %bitcast.59), kind=kOutput, calls=%fused_computation.9 | convolution fusion | flops 271580672 | bytes 8538112 | tf_op jit(solution)/shard_map/hrd,nhd->hrn/dot_general | solution.py:55
  30.2 0.0 copy-start.1
  30.2 1.9 %copy-done.1 = f32[8,64,2048]{2,1,0:T(8,128)} copy-done((f32[8,64,2048]{2,1,0:T(8,128)}, f32[8,64,2048]{2,1,0:T(8,128)S(1)}, u32[]{:S(2)}) %copy-start.1) | copy-done | bytes 4194328
  32.1 1.3 %convert_reduce_fusion = f32[8,64]{1,0:T(8,128)S(1)} fusion(f32[8,64]{1,0:T(8,128)S(1)} %compare_select_fusion, f32[8,64,2048]{2,1,0:T(8,128)S(1)} %get-tuple-element.13, pred[8,2048]{1,0:T(8,128)(4,1)S(1)} %broadcast_in_dim.48), kind=kLoop, calls=%fused_computation.6 | loop fusion | flops 7339520 | bytes 4214784 | tf_op jit(solution)/shard_map/reduce_sum | solution.py:65
  33.4 0.7 all_to_all.23
  34.1 3.5 %all-to-all-start.2 = ((f32[16,1,32]{2,1,0:T(1,128)}), f32[16,1,32]{2,1,0:T(1,128)S(1)}, u32[]{:S(2)}, u32[]{:S(2)}) async-start(f32[16,1,32]{2,1,0:T(1,128)} %all_to_all.23), calls=%async_computation.2 | async-start | bytes 16384 | tf_op jit(solution)/shard_map/all_to_all | solution.py:83
  37.6 0.0 copy-done
  37.7 0.6 gather_fusion
  38.2 0.2 fusion.6
  38.4 0.1 copy.37
  38.5 0.0 copy-start.2
  38.5 3.5 %copy.43 = bf16[256,8,8,128]{3,2,1,0:T(8,128)(2,1)S(1)} copy(bf16[256,8,8,128]{3,1,2,0:T(8,128)(2,1)} %bitcast.61) | data formatting | bytes 8388608
  42.0 0.0 copy-done.2
  42.0 0.0 copy-start.3
  42.0 2.5 %fusion = f32[8,64,128]{2,1,0:T(8,128)} fusion(bf16[2048,8,128]{2,1,0:T(8,128)(2,1)S(1)} %bitcast.62, f32[8,64,2048]{2,1,0:T(8,128)S(1)} %copy-done.2, f32[8,64]{1,0:T(8,128)S(1)} %compare_select_fusion, pred[8,2048]{1,0:T(8,128)(4,1)S(1)} %broadcast_in_dim.48), kind=kOutput, calls=%fused_computation.2 | convolution fusion | flops 273678336 | bytes 8669184 | tf_op jit(solution)/shard_map/hrn,nhd->hrd/dot_general | solution.py:66
  44.5 0.0 copy-done.3
  44.5 0.7 all_to_all.20
  45.2 0.0 all-to-all-done.2
  45.2 6.0 %all-to-all-start.1 = ((f32[16,1,32]{2,1,0:T(1,128)}), f32[16,1,32]{2,1,0:T(1,128)S(1)}, u32[]{:S(2)}, u32[]{:S(2)}) async-start(f32[16,1,32]{2,1,0:T(1,128)} %all_to_all.20), calls=%async_computation.1 | async-start | bytes 16384 | tf_op jit(solution)/shard_map/all_to_all | solution.py:82
  51.2 0.1 copy.38
  51.3 0.6 gather_fusion.1
  51.9 5.7 %all-to-all-done.1 = f32[16,1,32]{2,1,0:T(1,128)S(1)} async-done(((f32[16,1,32]{2,1,0:T(1,128)}), f32[16,1,32]{2,1,0:T(1,128)S(1)}, u32[]{:S(2)}, u32[]{:S(2)}) %all-to-all-start.1) | async-done | bytes 2080 | tf_op jit(solution)/shard_map/all_to_all | solution.py:82
  57.6 3.5 %all-to-all-start = ((f32[16,32,128]{2,1,0:T(8,128)}), f32[16,32,128]{2,1,0:T(8,128)S(1)}, u32[]{:S(2)}, u32[]{:S(2)}) async-start(f32[16,32,128]{2,1,0:T(8,128)} %bitcast.5), calls=%async_computation | async-start | bytes 524288 | tf_op jit(solution)/shard_map/all_to_all | solution.py:84
  61.1 0.2 fusion.15
  61.4 9.7 %all-to-all-done = f32[16,32,128]{2,1,0:T(8,128)S(1)} async-done(((f32[16,32,128]{2,1,0:T(8,128)}), f32[16,32,128]{2,1,0:T(8,128)S(1)}, u32[]{:S(2)}, u32[]{:S(2)}) %all-to-all-start) | async-done | bytes 262176 | tf_op jit(solution)/shard_map/all_to_all | solution.py:84
  71.1 0.1 multiply_reduce_fusion
  71.2 0.1 divide_convert_fusion
  71.3 18.9 %all_gather.7 = bf16[512,128]{1,0:T(8,128)(2,1)S(1)} all-gather(bf16[32,128]{1,0:T(8,128)(2,1)S(1)} %divide_convert_fusion), channel_id=1, replica_groups=mesh['grp'=2,'page'=16] {'page'}, dimensions={0}, use_global_device_ids=true | all-gather | bytes 139264 | tf_op jit(solution)/shard_map/all_gather | solution.py:101
  90.3 0.7 reshape.174
  (16 shorter events, 0.3 us)
Async XLA Ops:
  0.0 37.6 %copy-start = (bf16[16,1024]{1,0:T(8,128)(2,1)S(1)}, bf16[16,1024]{1,0:T(8,128)(2,1)}, u32[]{:S(2)}) copy-start(bf16[16,1024]{1,0:T(8,128)(2,1)} %param.9) | copy-start | bytes 98308
  30.2 1.9 %copy-start.1 = (f32[8,64,2048]{2,1,0:T(8,128)}, f32[8,64,2048]{2,1,0:T(8,128)S(1)}, u32[]{:S(2)}) copy-start(f32[8,64,2048]{2,1,0:T(8,128)S(1)} %get-tuple-element.13) | copy-start | bytes 12582916
  34.1 11.1 %all-to-all-start.2 = ((f32[16,1,32]{2,1,0:T(1,128)}), f32[16,1,32]{2,1,0:T(1,128)S(1)}, u32[]{:S(2)}, u32[]{:S(2)}) async-start(f32[16,1,32]{2,1,0:T(1,128)} %all_to_all.23), calls=%async_computation.2 | async-start | bytes 16384 | tf_op jit(solution)/shard_map/all_to_all | solution.py:83
  38.5 3.5 %copy-start.2 = (f32[8,64,2048]{2,1,0:T(8,128)S(1)}, f32[8,64,2048]{2,1,0:T(8,128)}, u32[]{:S(2)}) copy-start(f32[8,64,2048]{2,1,0:T(8,128)} %copy-done.1) | copy-start | bytes 12582916
  42.0 2.5 %copy-start.3 = (bf16[16,1024]{1,0:T(8,128)(2,1)S(1)}, bf16[16,1024]{1,0:T(8,128)(2,1)}, u32[]{:S(2)}) copy-start(bf16[16,1024]{1,0:T(8,128)(2,1)} %param.10) | copy-start | bytes 98308
  45.2 12.4 %all-to-all-start.1 = ((f32[16,1,32]{2,1,0:T(1,128)}), f32[16,1,32]{2,1,0:T(1,128)S(1)}, u32[]{:S(2)}, u32[]{:S(2)}) async-start(f32[16,1,32]{2,1,0:T(1,128)} %all_to_all.20), calls=%async_computation.1 | async-start | bytes 16384 | tf_op jit(solution)/shard_map/all_to_all | solution.py:82
  57.6 13.5 %all-to-all-start = ((f32[16,32,128]{2,1,0:T(8,128)}), f32[16,32,128]{2,1,0:T(8,128)S(1)}, u32[]{:S(2)}, u32[]{:S(2)}) async-start(f32[16,32,128]{2,1,0:T(8,128)} %bitcast.5), calls=%async_computation | async-start | bytes 524288 | tf_op jit(solution)/shard_map/all_to_all | solution.py:84
where the time goes:
time: 91.4 us; the launch traced here: 91 us
  blocking collectives  42.5 us (46%)
  waiting for transfers between devices  15.5 us (17%)
  local copies, waits for them, and re-layouts  13.5 us (15%)
  starting transfers between devices  13 us (14%)
  matrix products  4.53 us (5%)
  other arithmetic  1.9 us (2%)
    all_gather x1, blocking collectives, on_device(): chosen_all = lax.all_gather(chosen, 'page', axis=1, tiled=True)  23.5 us
    all_gather x1, blocking collectives, on_device(): result = lax.all_gather(finished, 'page', axis=0, tiled=True)  18.9 us
    all_to_all x1, waiting for transfers between devices, on_device(): lax.all_to_all(pieces[2], 'page', split_axis=0, concat_axis=0, tiled=True)  9.74 us
    unnamed x10, local copies, waits for them, and re-layouts  8.68 us
    all_to_all x1, starting transfers between devices, on_device(): lax.all_to_all(pieces[0], 'page', split_axis=0, concat_axis=0, tiled=True)  5.97 us
    all_to_all x1, waiting for transfers between devices, on_device(): lax.all_to_all(pieces[0], 'page', split_axis=0, concat_axis=0, tiled=True)  5.72 us
    all_to_all x1, starting transfers between devices, on_device(): lax.all_to_all(pieces[2], 'page', split_axis=0, concat_axis=0, tiled=True)  3.53 us
    all_to_all x1, starting transfers between devices, on_device(): lax.all_to_all(pieces[1], 'page', split_axis=0, concat_axis=0, tiled=True)  3.47 us
  transfers between devices with their start and end apart: 3, of which 2 were waited for; matrix products, arithmetic and copies ran while one was open for 9% of the time, Pallas kernels for 0%

commit v1 on v0

v1 whole, which is shorter than its diff:
```python
import functools

import jax
import jax.numpy as jnp
from jax import lax
from jax.experimental import pallas as pl
from jax.experimental.pallas import tpu as pltpu
from jax.sharding import PartitionSpec as P

LOW = -1e30
LOG2E = 1.4426950408889634
LANES = 128
BF16 = jnp.bfloat16
F32 = jnp.float32


def dot(a, b, dims):
    return lax.dot_general(a, b, (dims, ((), ())), preferred_element_type=F32)


def kernel(
    n, owners, kv_heads, groups,
    queries, key_hbm, value_hbm, new_keys, new_values, chosen, out_ref,
    kbuf, vbuf, qbd, weights, page_high, page_sums, gbuf, gsend,
    obuf, sbuf, orecv, srecv, factors, fin, finrecv,
    load_sem, g_send, g_recv, o_send, o_recv, s_send, s_recv, f_send, f_recv,
):
    me = lax.axis_index("page")
    pages, tokens, span = key_hbm.shape
    width = span // kv_heads
    drafts = queries.shape[0]
    pairs = kv_heads // 2
    rows = drafts * groups
    heads = kv_heads * groups
    per_owner = heads // owners
    per_pair = 2 * groups
    rate = width ** (-0.5) * LOG2E
    everyone = owners == n

    def peer_of(k):
        return lax.rem(me + k, n)

    loads = []
    for j in range(pairs):
        cols = pl.ds(j * 2 * width, 2 * width)
        loads.append((
            pltpu.make_async_copy(key_hbm.at[:, :, cols], kbuf.at[j], load_sem.at[0, j]),
            pltpu.make_async_copy(value_hbm.at[:, :, cols], vbuf.at[j], load_sem.at[1, j]),
        ))
    for key_load, _ in loads:
        key_load.start()
    for _, value_load in loads:
        value_load.start()

    barrier = pltpu.get_barrier_semaphore()

    def greet(k, carry):
        pl.semaphore_signal(barrier, inc=1, device_id={"page": peer_of(k)},
                            device_id_type=pl.DeviceIdType.MESH)
        return carry

    lax.fori_loop(1, n, greet, 0)

    per = chosen.shape[1]
    slots = LANES // per
    lane_ids = lax.broadcasted_iota(jnp.int32, (kv_heads, LANES), 1)
    tiled = jnp.concatenate([chosen[...]] * slots, axis=1)
    mine = jnp.where(lane_ids // per == lax.rem(me, slots), tiled, -1)
    gsend[...] = mine
    gbuf[pl.ds(me, 1)] = mine[None]

    blank = jnp.zeros((rows, width), BF16)
    for j in range(pairs):
        parts = []
        for a in range(2):
            head = 2 * j + a
            stack = jnp.concatenate(
                [queries[:, (head * groups + g) * width:(head * groups + g + 1) * width]
                 for g in range(groups)], axis=0)
            parts.append(jnp.concatenate([stack, blank] if a == 0 else [blank, stack], axis=1))
        qbd[j] = jnp.concatenate(parts, axis=0)

    pl.semaphore_wait(barrier, n - 1)

    def g_copy(k, target, slot):
        return pltpu.make_async_remote_copy(
            src_ref=gsend, dst_ref=gbuf.at[slot], send_sem=g_send.at[k], recv_sem=g_recv.at[slot],
            device_id={"page": target}, device_id_type=pl.DeviceIdType.MESH)

    def g_start(k, carry):
        g_copy(k, peer_of(k), me).start()
        return carry

    lax.fori_loop(1, n, g_start, 0)

    step = 4
    for j in range(pairs):
        loads[j][0].wait()
        for p in range(0, pages, step):
            keys = kbuf[j, p:p + step].reshape(step * tokens, 2 * width)
            scores = dot(keys, qbd[j], ((1,), (1,)))
            for i in range(step):
                part = scores[i * tokens:(i + 1) * tokens]
                high = jnp.max(part, axis=0, keepdims=True)
                raised = jnp.exp2((part - high) * rate)
                page_high[j, p + i:p + i + 1] = high
                page_sums[j, p + i:p + i + 1] = jnp.sum(raised, axis=0, keepdims=True)
                weights[j, p + i] = raised.astype(BF16)

    first = me * per_owner
    lanes = lax.broadcasted_iota(jnp.int32, (drafts, 2 * rows), 1)
    keys_at = lax.broadcasted_iota(jnp.int32, (drafts, 2 * rows), 0)
    fresh = []
    for j in range(pairs):
        cols = slice(j * 2 * width, (j + 1) * 2 * width)
        scores = dot(new_keys[:, cols], qbd[j], ((1,), (1,)))
        head_of = lanes // drafts + j * per_pair
        ok = (keys_at <= lanes % drafts) & (head_of >= first) & (head_of < first + per_owner)
        high = jnp.max(jnp.where(ok, scores, LOW), axis=0, keepdims=True)
        raised = jnp.where(ok, jnp.exp2((scores - high) * rate), 0.0)
        fresh.append((high, jnp.sum(raised, axis=0, keepdims=True), raised))

    def g_wait(k, carry):
        copy = g_copy(k, peer_of(k), peer_of(k))
        copy.wait_recv()
        copy.wait_send()
        return carry

    lax.fori_loop(1, n, g_wait, 0)

    named = [jnp.max(gbuf[t * slots:(t + 1) * slots], axis=0) for t in range(n // slots)]
    page_ids = lax.broadcasted_iota(jnp.int32, (pages, LANES), 0) + me * pages
    picked = []
    for h in range(kv_heads):
        hit = named[0][h:h + 1] == page_ids
        for other in named[1:]:
            hit = hit | (other[h:h + 1] == page_ids)
        picked.append(jnp.max(jnp.where(hit, 1.0, 0.0), axis=1, keepdims=True))
    pair_lanes = lax.broadcasted_iota(jnp.int32, (pages, 2 * rows), 1)

    def o_copy(k, target, slot, owner):
        return pltpu.make_async_remote_copy(
            src_ref=obuf.at[pl.ds(owner * per_owner, per_owner)], dst_ref=orecv.at[slot],
            send_sem=o_send.at[k], recv_sem=o_recv.at[slot],
            device_id={"page": target}, device_id_type=pl.DeviceIdType.MESH)

    def s_copy(k, target, slot, owner):
        return pltpu.make_async_remote_copy(
            src_ref=sbuf.at[owner * per_owner // per_pair], dst_ref=srecv.at[slot],
            send_sem=s_send.at[k], recv_sem=s_recv.at[slot],
            device_id={"page": target}, device_id_type=pl.DeviceIdType.MESH)

    wide = 8
    for j in range(pairs):
        in_use = jnp.where(pair_lanes < rows, picked[2 * j], picked[2 * j + 1]) > 0.5
        high_fresh, sums_fresh, raised_fresh = fresh[j]
        highs = page_high[j]
        top = jnp.maximum(jnp.max(jnp.where(in_use, highs, LOW), axis=0, keepdims=True), high_fresh)
        share = jnp.where(in_use, jnp.exp2((highs - top) * rate), 0.0).astype(BF16)
        share_fresh = jnp.exp2((high_fresh - top) * rate)
        total = jnp.sum(share.astype(F32) * page_sums[j], axis=0, keepdims=True)
        total = total + share_fresh * sums_fresh
        loads[j][1].wait()
        acc = dot((raised_fresh * share_fresh).astype(BF16),
                  new_values[:, j * 2 * width:(j + 1) * 2 * width], ((0,), (0,)))
        for p in range(0, pages, wide):
            scaled = weights[j, p:p + wide] * share[p:p + wide][:, None, :]
            acc = acc + dot(scaled.reshape(wide * tokens, 2 * rows),
                            vbuf[j, p:p + wide].reshape(wide * tokens, 2 * width), ((0,), (0,)))
        sbuf[j, 0:1] = top
        sbuf[j, 1:2] = total
        for a in range(2):
            part = acc[a * rows:(a + 1) * rows, a * width:(a + 1) * width].astype(BF16)
            obuf[(2 * j + a) * groups:(2 * j + a + 1) * groups] = part.reshape(groups, drafts, width)

        owned = per_pair // per_owner
        for o in range(j * owned, (j + 1) * owned):
            @pl.when(me != o)
            def _():
                s_copy(o, o, me, o).start()
                o_copy(o, o, me, o).start()

    def f_copy(k, target, slot):
        return pltpu.make_async_remote_copy(
            src_ref=fin, dst_ref=finrecv.at[slot], send_sem=f_send.at[k], recv_sem=f_recv.at[slot],
            device_id={"page": target}, device_id_type=pl.DeviceIdType.MESH)

    def finish():
        srecv[pl.ds(me, 1)] = sbuf[pl.ds(me * per_owner // per_pair, 1)]
        orecv[pl.ds(me, 1)] = obuf[pl.ds(first, per_owner)][None]

        def s_wait(k, carry):
            s_copy(peer_of(k), peer_of(k), peer_of(k), me).wait_recv()
            return carry

        lax.fori_loop(1, n, s_wait, 0)
        highs = srecv[:, 0, :]
        top = jnp.max(highs, axis=0, keepdims=True)
        share = jnp.exp2((highs - top) * rate)
        total = jnp.sum(share * srecv[:, 1, :], axis=0, keepdims=True)
        factors[...] = jnp.transpose(share / total)
        own_rows = per_owner * drafts
        own = factors[pl.ds(pl.multiple_of(lax.rem(first, per_pair) * drafts, drafts), own_rows), :]

        def o_wait(k, carry):
            o_copy(peer_of(k), peer_of(k), peer_of(k), me).wait_recv()
            return carry

        lax.fori_loop(1, n, o_wait, 0)
        acc = jnp.zeros((own_rows, width), F32)
        for i in range(n):
            acc = acc + own[:, i:i + 1] * orecv[i].reshape(own_rows, width).astype(F32)
        done = acc.astype(BF16).reshape(per_owner, drafts, width)
        fin[...] = done
        finrecv[pl.ds(me, 1)] = done[None]

        def f_start(k, carry):
            f_copy(k, peer_of(k), me).start()
            return carry

        lax.fori_loop(1, n, f_start, 0)

    if everyone:
        finish()
    else:
        pl.when(me < owners)(finish)

    def sent(o, carry):
        @pl.when(me != o)
        def _():
            s_copy(o, o, me, o).wait_send()
            o_copy(o, o, me, o).wait_send()
        return carry

    lax.fori_loop(0, owners, sent, 0)

    def f_wait(o, carry):
        @pl.when(me != o)
        def _():
            f_copy(o, o, o).wait_recv()
        return carry

    lax.fori_loop(0, owners, f_wait, 0)
    for o in range(owners):
        for i in range(per_owner):
            head = o * per_owner + i
            out_ref[:, head * width:(head + 1) * width] = finrecv[o, i]

    def f_sent():
        def body(k, carry):
            f_copy(k, peer_of(k), me).wait_send()
            return carry

        lax.fori_loop(1, n, body, 0)

    if everyone:
        f_sent()
    else:
        pl.when(me < owners)(f_sent)


def on_device(queries, key_cache, value_cache, new_keys, new_values, chosen):
    n = lax.axis_size("page")
    pages, tokens, span = key_cache.shape
    drafts = queries.shape[0]
    groups = queries.shape[1] // span
    kv_heads = chosen.shape[0]
    width = span // kv_heads
    pairs = kv_heads // 2
    heads = kv_heads * groups
    rows = drafts * groups
    owners = min(n, heads)
    per_owner = heads // owners
    vmem = pl.BlockSpec(memory_space=pltpu.VMEM)
    hbm = pl.BlockSpec(memory_space=pl.ANY)
    dma = pltpu.SemaphoreType.DMA
    return pl.pallas_call(
        functools.partial(kernel, n, owners, kv_heads, groups),
        out_shape=jax.ShapeDtypeStruct(queries.shape, BF16),
        in_specs=[vmem, hbm, hbm, vmem, vmem, vmem],
        out_specs=vmem,
        scratch_shapes=[
            pltpu.VMEM((pairs, pages, tokens, 2 * width), BF16),
            pltpu.VMEM((pairs, pages, tokens, 2 * width), BF16),
            pltpu.VMEM((pairs, 2 * rows, 2 * width), BF16),
            pltpu.VMEM((pairs, pages, tokens, 2 * rows), BF16),
            pltpu.VMEM((pairs, pages, 2 * rows), F32),
            pltpu.VMEM((pairs, pages, 2 * rows), F32),
            pltpu.VMEM((n, kv_heads, LANES), jnp.int32),
            pltpu.VMEM((kv_heads, LANES), jnp.int32),
            pltpu.VMEM((heads, drafts, width), BF16),
            pltpu.VMEM((pairs, 2, 2 * rows), F32),
            pltpu.VMEM((n, per_owner, drafts, width), BF16),
            pltpu.VMEM((n, 2, 2 * rows), F32),
            pltpu.VMEM((2 * rows, n), F32),
            pltpu.VMEM((per_owner, drafts, width), BF16),
            pltpu.VMEM((owners, per_owner, drafts, width), BF16),
            dma((2, pairs)),
            dma((n,)), dma((n,)),
            dma((n,)), dma((n,)),
            dma((n,)), dma((n,)),
            dma((n,)), dma((n,)),
        ],
        compiler_params=pltpu.CompilerParams(collective_id=0, has_side_effects=True),
        name="paged_attention",
    )(queries, key_cache, value_cache, new_keys, new_values, chosen)


def solution(mesh):
    placed = (
        P("grp", None),
        P(("grp", "page"), None, None),
        P(("grp", "page"), None, None),
        P("grp", None),
        P("grp", None),
        P("grp", "page"),
    )
    return jax.shard_map(
        on_device, mesh=mesh, in_specs=placed, out_specs=P("grp", None), check_vma=False
    )
```

time: 91.4 us -> 25.7 us (0.28)
  blocking collectives: 42.5 us -> 0 us
  Pallas kernels: 0 us -> 23.9 us
  waiting for transfers between devices: 15.5 us -> 0 us
  starting transfers between devices: 13 us -> 0 us
  local copies, waits for them, and re-layouts: 13.5 us -> 1.57 us
  matrix products: 4.53 us -> 0 us
  other arithmetic: 1.9 us -> 0 us
    all_gather x2 -> x0, blocking collectives: 42.5 us -> none  [the longest x1 23.5 us: on_device(): chosen_all = lax.all_gather(chosen, 'page', axis=1, tiled=True)]
    pallas_call x0 -> x1, Pallas kernels: none -> 23.9 us  [on_device(): pl.pallas_call(functools.partial(kernel, n, owners, kv_heads, groups), ou...]
    all_to_all x3 -> x0, waiting for transfers between devices: 15.5 us -> none  [the longest x1 9.74 us: on_device(): lax.all_to_all(pieces[2], 'page', split_axis=0, concat_axis=0, tiled=True)]
    all_to_all x3 -> x0, starting transfers between devices: 13 us -> none  [the longest x1 5.97 us: on_device(): lax.all_to_all(pieces[0], 'page', split_axis=0, concat_axis=0, tiled=True)]
    unnamed x10 -> x1, local copies, waits for them, and re-layouts: 8.68 us -> 1.57 us
    dot_general x4 -> x0, matrix products: 4.53 us -> none  [the longest x1 2.46 us: on_device(): jnp.einsum('hrn,nhd->hrd', weights, value_flat, preferred_element_type=jn...]
    reshape x3 -> x0, local copies, waits for them, and re-layouts: 1.76 us -> none  [the longest x2 1.03 us: on_device(): queries.reshape(drafts, kv_heads, groups, head_width).transpose(1, 0, 2, 3)]
    reduce_sum x4 -> x0, other arithmetic: 1.48 us -> none  [the longest x1 1.3 us: on_device(): totals = jnp.sum(weights.astype(jnp.float32), axis=2)]
  transfers between devices with their start and end apart: 3 -> 0, of which waited for: 2 -> 0; matrix products, arithmetic and copies ran while one was open for 9% -> 0% of each run, Pallas kernels for 0% -> 0%
where the time goes in v1:
time: 25.7 us; the launch traced here: 25.5 us
  Pallas kernels  23.9 us (93%)
  local copies, waits for them, and re-layouts  1.57 us (6%)
    pallas_call x1, Pallas kernels, on_device(): pl.pallas_call(functools.partial(kernel, n, owners, kv_heads, groups), ou...  23.9 us
    unnamed x1, local copies, waits for them, and re-layouts  1.57 us

profile of v1, /device:TPU:0, one launch (start us, length us, event | category | flops | bytes accessed | tf_op | source)
XLA Modules:
  0.0 25.5 jit_solution(1307517900250074409)
XLA Ops:
  0.0 23.9 %paged_attention.1 = bf16[16,4096]{1,0:T(8,128)(2,1)} custom-call(bf16[16,4096]{1,0:T(8,128)(2,1)} %queries.1, bf16[32,64,1024]{2,1,0:T(8,128)(2,1)} %key_hbm.1, bf16[32,64,1024]{2,1,0:T(8,128)(2,1)} %value_hbm.1, bf16[16,1024]{1,0:T(8,128)(2,1)} %new_keys.1, bf16[16,1024]{1,0:T(8,128)(2,1)} %new_values.1, s32[8,16]{1,0:T(8,128)} %chosen.1), custom_call_target="tpu_custom_call" | custom-call | tf_op jit(solution)/shard_map/paged_attention/pallas_call | solution.py:277
  24.0 1.6 %copy.8 = bf16[16,4096]{1,0:T(8,128)(2,1)} copy(bf16[16,4096]{1,0:T(8,128)(2,1)} %paged_attention.1) | data formatting | bytes 262144

commit v2 on v1

--- a/solution.py
+++ b/solution.py
@@ -20,10 +20,10 @@
 
 def kernel(
     n, owners, kv_heads, groups,
-    queries, key_hbm, value_hbm, new_keys, new_values, chosen, out_ref,
-    kbuf, vbuf, qbd, weights, page_high, page_sums, gbuf, gsend,
-    obuf, sbuf, orecv, srecv, factors, fin, finrecv,
-    load_sem, g_send, g_recv, o_send, o_recv, s_send, s_recv, f_send, f_recv,
+    queries_hbm, key_hbm, value_hbm, new_keys_hbm, new_values_hbm, chosen_hbm, out_ref,
+    queries, new_keys, new_values, chosen, kbuf, vbuf, qbd, weights, page_high, page_sums, gbuf, gsend,
+    obuf, sbuf, orecv, srecv, factors, fin,
+    small_sem, load_sem, g_send, g_recv, o_send, o_recv, s_send, s_recv, f_send, f_recv,
 ):
     me = lax.axis_index("page")
     pages, tokens, span = key_hbm.shape
@@ -40,6 +40,23 @@
     def peer_of(k):
         return lax.rem(me + k, n)
 
+    barrier = pltpu.get_barrier_semaphore()
+
+    def greet(k, carry):
+        pl.semaphore_signal(barrier, inc=1, device_id={"page": peer_of(k)},
+                            device_id_type=pl.DeviceIdType.MESH)
+        return carry
+
+    lax.fori_loop(1, n, greet, 0)
+
+    small = [
+        pltpu.make_async_copy(src, dst, small_sem.at[i])
+        for i, (src, dst) in enumerate((
+            (chosen_hbm, chosen), (queries_hbm, queries),
+            (new_keys_hbm, new_keys), (new_values_hbm, new_values)))
+    ]
+    small[0].start()
+    small[1].start()
     loads = []
     for j in range(pairs):
         cols = pl.ds(j * 2 * width, 2 * width)
@@ -51,24 +68,32 @@
         key_load.start()
     for _, value_load in loads:
         value_load.start()
-
-    barrier = pltpu.get_barrier_semaphore()
-
-    def greet(k, carry):
-        pl.semaphore_signal(barrier, inc=1, device_id={"page": peer_of(k)},
-                            device_id_type=pl.DeviceIdType.MESH)
-        return carry
-
-    lax.fori_loop(1, n, greet, 0)
+    small[2].start()
+    small[3].start()
 
     per = chosen.shape[1]
     slots = LANES // per
     lane_ids = lax.broadcasted_iota(jnp.int32, (kv_heads, LANES), 1)
+    small[0].wait()
     tiled = jnp.concatenate([chosen[...]] * slots, axis=1)
     mine = jnp.where(lane_ids // per == lax.rem(me, slots), tiled, -1)
     gsend[...] = mine
     gbuf[pl.ds(me, 1)] = mine[None]
 
+    pl.semaphore_wait(barrier, n - 1)
+
+    def g_copy(k, target, slot):
+        return pltpu.make_async_remote_copy(
+            src_ref=gsend, dst_ref=gbuf.at[slot], send_sem=g_send.at[k], recv_sem=g_recv.at[slot],
+            device_id={"page": target}, device_id_type=pl.DeviceIdType.MESH)
+
+    def g_start(k, carry):
+        g_copy(k, peer_of(k), me).start()
+        return carry
+
+    lax.fori_loop(1, n, g_start, 0)
+
+    small[1].wait()
     blank = jnp.zeros((rows, width), BF16)
     for j in range(pairs):
         parts = []
@@ -80,19 +105,6 @@
             parts.append(jnp.concatenate([stack, blank] if a == 0 else [blank, stack], axis=1))
         qbd[j] = jnp.concatenate(parts, axis=0)
 
-    pl.semaphore_wait(barrier, n - 1)
-
-    def g_copy(k, target, slot):
-        return pltpu.make_async_remote_copy(
-            src_ref=gsend, dst_ref=gbuf.at[slot], send_sem=g_send.at[k], recv_sem=g_recv.at[slot],
-            device_id={"page": target}, device_id_type=pl.DeviceIdType.MESH)
-
-    def g_start(k, carry):
-        g_copy(k, peer_of(k), me).start()
-        return carry
-
-    lax.fori_loop(1, n, g_start, 0)
-
     step = 4
     for j in range(pairs):
         loads[j][0].wait()
@@ -101,8 +113,8 @@
             scores = dot(keys, qbd[j], ((1,), (1,)))
             for i in range(step):
                 part = scores[i * tokens:(i + 1) * tokens]
-                high = jnp.max(part, axis=0, keepdims=True)
-                raised = jnp.exp2((part - high) * rate)
+                high = jnp.ceil(jnp.max(part, axis=0, keepdims=True) * rate)
+                raised = jnp.exp2(part * rate - high)
                 page_high[j, p + i:p + i + 1] = high
                 page_sums[j, p + i:p + i + 1] = jnp.sum(raised, axis=0, keepdims=True)
                 weights[j, p + i] = raised.astype(BF16)
@@ -111,13 +123,15 @@
     lanes = lax.broadcasted_iota(jnp.int32, (drafts, 2 * rows), 1)
     keys_at = lax.broadcasted_iota(jnp.int32, (drafts, 2 * rows), 0)
     fresh = []
+    small[2].wait()
+    small[3].wait()
     for j in range(pairs):
         cols = slice(j * 2 * width, (j + 1) * 2 * width)
         scores = dot(new_keys[:, cols], qbd[j], ((1,), (1,)))
         head_of = lanes // drafts + j * per_pair
         ok = (keys_at <= lanes % drafts) & (head_of >= first) & (head_of < first + per_owner)
-        high = jnp.max(jnp.where(ok, scores, LOW), axis=0, keepdims=True)
-        raised = jnp.where(ok, jnp.exp2((scores - high) * rate), 0.0)
+        high = jnp.ceil(jnp.max(jnp.where(ok, scores * rate, LOW), axis=0, keepdims=True))
+        raised = jnp.where(ok, jnp.exp2(scores * rate - high), 0.0)
         fresh.append((high, jnp.sum(raised, axis=0, keepdims=True), raised))
 
     def g_wait(k, carry):
@@ -156,8 +170,8 @@
         high_fresh, sums_fresh, raised_fresh = fresh[j]
         highs = page_high[j]
         top = jnp.maximum(jnp.max(jnp.where(in_use, highs, LOW), axis=0, keepdims=True), high_fresh)
-        share = jnp.where(in_use, jnp.exp2((highs - top) * rate), 0.0).astype(BF16)
-        share_fresh = jnp.exp2((high_fresh - top) * rate)
+        share = jnp.where(in_use, jnp.exp2(highs - top), 0.0).astype(BF16)
+        share_fresh = jnp.exp2(high_fresh - top)
         total = jnp.sum(share.astype(F32) * page_sums[j], axis=0, keepdims=True)
         total = total + share_fresh * sums_fresh
         loads[j][1].wait()
@@ -180,9 +194,13 @@
                 s_copy(o, o, me, o).start()
                 o_copy(o, o, me, o).start()
 
+    def block_of(owner):
+        cols = per_owner * width
+        return out_ref.at[:, pl.ds(pl.multiple_of(owner * cols, cols), cols)]
+
     def f_copy(k, target, slot):
         return pltpu.make_async_remote_copy(
-            src_ref=fin, dst_ref=finrecv.at[slot], send_sem=f_send.at[k], recv_sem=f_recv.at[slot],
+            src_ref=fin, dst_ref=block_of(slot), send_sem=f_send.at[k], recv_sem=f_recv.at[slot],
             device_id={"page": target}, device_id_type=pl.DeviceIdType.MESH)
 
     def finish():
@@ -196,7 +214,7 @@
         lax.fori_loop(1, n, s_wait, 0)
         highs = srecv[:, 0, :]
         top = jnp.max(highs, axis=0, keepdims=True)
-        share = jnp.exp2((highs - top) * rate)
+        share = jnp.exp2(highs - top)
         total = jnp.sum(share * srecv[:, 1, :], axis=0, keepdims=True)
         factors[...] = jnp.transpose(share / total)
         own_rows = per_owner * drafts
@@ -210,15 +228,16 @@
         acc = jnp.zeros((own_rows, width), F32)
         for i in range(n):
             acc = acc + own[:, i:i + 1] * orecv[i].reshape(own_rows, width).astype(F32)
-        done = acc.astype(BF16).reshape(per_owner, drafts, width)
-        fin[...] = done
-        finrecv[pl.ds(me, 1)] = done[None]
+        done = acc.astype(BF16)
+        for i in range(per_owner):
+            fin[:, i * width:(i + 1) * width] = done[i * drafts:(i + 1) * drafts]
 
         def f_start(k, carry):
             f_copy(k, peer_of(k), me).start()
             return carry
 
         lax.fori_loop(1, n, f_start, 0)
+        block_of(me)[...] = fin[...]
 
     if everyone:
         finish()
@@ -241,11 +260,6 @@
         return carry
 
     lax.fori_loop(0, owners, f_wait, 0)
-    for o in range(owners):
-        for i in range(per_owner):
-            head = o * per_owner + i
-            out_ref[:, head * width:(head + 1) * width] = finrecv[o, i]
-
     def f_sent():
         def body(k, carry):
             f_copy(k, peer_of(k), me).wait_send()
@@ -276,10 +290,14 @@
     dma = pltpu.SemaphoreType.DMA
     return pl.pallas_call(
         functools.partial(kernel, n, owners, kv_heads, groups),
-        out_shape=jax.ShapeDtypeStruct(queries.shape, BF16),
-        in_specs=[vmem, hbm, hbm, vmem, vmem, vmem],
+        out_shape=pltpu.VMEM(queries.shape, BF16),
+        in_specs=[hbm] * 6,
         out_specs=vmem,
         scratch_shapes=[
+            pltpu.VMEM(queries.shape, BF16),
+            pltpu.VMEM(new_keys.shape, BF16),
+            pltpu.VMEM(new_values.shape, BF16),
+            pltpu.VMEM(chosen.shape, jnp.int32),
             pltpu.VMEM((pairs, pages, tokens, 2 * width), BF16),
             pltpu.VMEM((pairs, pages, tokens, 2 * width), BF16),
             pltpu.VMEM((pairs, 2 * rows, 2 * width), BF16),
@@ -293,9 +311,8 @@
             pltpu.VMEM((n, per_owner, drafts, width), BF16),
             pltpu.VMEM((n, 2, 2 * rows), F32),
             pltpu.VMEM((2 * rows, n), F32),
-            pltpu.VMEM((per_owner, drafts, width), BF16),
-            pltpu.VMEM((owners, per_owner, drafts, width), BF16),
-            dma((2, pairs)),
+            pltpu.VMEM((drafts, per_owner * width), BF16),
+            dma((4,)), dma((2, pairs)),
             dma((n,)), dma((n,)),
             dma((n,)), dma((n,)),
             dma((n,)), dma((n,)),

time: 25.7 us -> 24 us (0.934)
  local copies, waits for them, and re-layouts: 1.57 us -> 0.66 us
  Pallas kernels: 23.9 us -> 23.2 us
    unnamed x1, local copies, waits for them, and re-layouts: 1.57 us -> 0.66 us
    pallas_call x1, Pallas kernels: 23.9 us -> 23.2 us  [on_device(): pl.pallas_call(functools.partial(kernel, n, owners, kv_heads, groups), ou...]
where the time goes in v2:
time: 24 us; the launch traced here: 23.8 us
  Pallas kernels  23.2 us (97%)
  local copies, waits for them, and re-layouts  0.66 us (3%)
    pallas_call x1, Pallas kernels, on_device(): pl.pallas_call(functools.partial(kernel, n, owners, kv_heads, groups), ou...  23.2 us
    unnamed x1, local copies, waits for them, and re-layouts  0.66 us

profile of v2, /device:TPU:0, one launch (start us, length us, event | category | flops | bytes accessed | tf_op | source)
XLA Modules:
  0.0 23.8 jit_solution(6910912027162894249)
XLA Ops:
  0.0 23.2 %paged_attention.1 = bf16[16,4096]{1,0:T(8,128)(2,1)S(1)} custom-call(bf16[16,4096]{1,0:T(8,128)(2,1)} %queries_hbm.1, bf16[32,64,1024]{2,1,0:T(8,128)(2,1)} %key_hbm.1, bf16[32,64,1024]{2,1,0:T(8,128)(2,1)} %value_hbm.1, bf16[16,1024]{1,0:T(8,128)(2,1)} %new_keys_hbm.1, bf16[16,1024]{1,0:T(8,128)(2,1)} %new_values_hbm.1, s32[8,16]{1,0:T(8,128)} %chosen_hbm.1), custom_call_target="tpu_custom_call" | custom-call | tf_op jit(solution)/shard_map/paged_attention/pallas_call | solution.py:291
  23.2 0.7 %copy.8 = bf16[16,4096]{1,0:T(8,128)(2,1)} copy(bf16[16,4096]{1,0:T(8,128)(2,1)S(1)} %paged_attention.1) | data formatting | bytes 262144

commit v3 on v2

--- a/solution.py
+++ b/solution.py
@@ -114,10 +114,10 @@
             for i in range(step):
                 part = scores[i * tokens:(i + 1) * tokens]
                 high = jnp.ceil(jnp.max(part, axis=0, keepdims=True) * rate)
-                raised = jnp.exp2(part * rate - high)
+                raised = jnp.exp2(part * rate - high).astype(BF16)
                 page_high[j, p + i:p + i + 1] = high
-                page_sums[j, p + i:p + i + 1] = jnp.sum(raised, axis=0, keepdims=True)
-                weights[j, p + i] = raised.astype(BF16)
+                page_sums[j, p + i:p + i + 1] = jnp.sum(raised.astype(F32), axis=0, keepdims=True)
+                weights[j, p + i] = raised
 
     first = me * per_owner
     lanes = lax.broadcasted_iota(jnp.int32, (drafts, 2 * rows), 1)
@@ -131,7 +131,7 @@
         head_of = lanes // drafts + j * per_pair
         ok = (keys_at <= lanes % drafts) & (head_of >= first) & (head_of < first + per_owner)
         high = jnp.ceil(jnp.max(jnp.where(ok, scores * rate, LOW), axis=0, keepdims=True))
-        raised = jnp.where(ok, jnp.exp2(scores * rate - high), 0.0)
+        raised = jnp.where(ok, jnp.exp2(scores * rate - high), 0.0).astype(BF16).astype(F32)
         fresh.append((high, jnp.sum(raised, axis=0, keepdims=True), raised))
 
     def g_wait(k, carry):

time: 24 us -> 24 us (level)
  no operation moved by 1% of the time
where the time goes in v3:
time: 24 us; the launch traced here: 23.8 us
  Pallas kernels  23.2 us (97%)
  local copies, waits for them, and re-layouts  0.66 us (3%)
    pallas_call x1, Pallas kernels, on_device(): pl.pallas_call(functools.partial(kernel, n, owners, kv_heads, groups), ou...  23.2 us
    unnamed x1, local copies, waits for them, and re-layouts  0.66 us

profile of v3, /device:TPU:0, one launch (start us, length us, event | category | flops | bytes accessed | tf_op | source)
XLA Modules:
  0.0 23.8 jit_solution(9673184857128857445)
XLA Ops:
  0.0 23.2 %paged_attention.1 = bf16[16,4096]{1,0:T(8,128)(2,1)S(1)} custom-call(bf16[16,4096]{1,0:T(8,128)(2,1)} %queries_hbm.1, bf16[32,64,1024]{2,1,0:T(8,128)(2,1)} %key_hbm.1, bf16[32,64,1024]{2,1,0:T(8,128)(2,1)} %value_hbm.1, bf16[16,1024]{1,0:T(8,128)(2,1)} %new_keys_hbm.1, bf16[16,1024]{1,0:T(8,128)(2,1)} %new_values_hbm.1, s32[8,16]{1,0:T(8,128)} %chosen_hbm.1), custom_call_target="tpu_custom_call" | custom-call | tf_op jit(solution)/shard_map/paged_attention/pallas_call | solution.py:291
  23.2 0.7 %copy.8 = bf16[16,4096]{1,0:T(8,128)(2,1)} copy(bf16[16,4096]{1,0:T(8,128)(2,1)S(1)} %paged_attention.1) | data formatting | bytes 262144

commit v4 on v3

--- a/solution.py
+++ b/solution.py
@@ -21,7 +21,7 @@
 def kernel(
     n, owners, kv_heads, groups,
     queries_hbm, key_hbm, value_hbm, new_keys_hbm, new_values_hbm, chosen_hbm, out_ref,
-    queries, new_keys, new_values, chosen, kbuf, vbuf, qbd, weights, page_high, page_sums, gbuf, gsend,
+    queries, new_keys, new_values, chosen, kbuf, vbuf, qbd, weights, page_high, page_sums, gbuf, gsend, picked, fresh_stats, fresh_weights,
     obuf, sbuf, orecv, srecv, factors, fin,
     small_sem, load_sem, g_send, g_recv, o_send, o_recv, s_send, s_recv, f_send, f_recv,
 ):
@@ -40,6 +40,14 @@
     def peer_of(k):
         return lax.rem(me + k, n)
 
+    def far_first(count, act):
+        def body(k, carry):
+            peer = jnp.where(me * 2 < n, count - 1 - k, k)
+            pl.when(peer != me)(lambda: act(peer))
+            return carry
+
+        lax.fori_loop(0, count, body, 0)
+
     barrier = pltpu.get_barrier_semaphore()
 
     def greet(k, carry):
@@ -72,11 +80,11 @@
     small[3].start()
 
     per = chosen.shape[1]
-    slots = LANES // per
-    lane_ids = lax.broadcasted_iota(jnp.int32, (kv_heads, LANES), 1)
     small[0].wait()
-    tiled = jnp.concatenate([chosen[...]] * slots, axis=1)
-    mine = jnp.where(lane_ids // per == lax.rem(me, slots), tiled, -1)
+    pieces = [chosen[h:h + 1, :] for h in range(kv_heads)]
+    if kv_heads * per < LANES:
+        pieces.append(jnp.full((1, LANES - kv_heads * per), -1, jnp.int32))
+    mine = jnp.concatenate(pieces, axis=1)
     gsend[...] = mine
     gbuf[pl.ds(me, 1)] = mine[None]
 
@@ -87,11 +95,7 @@
             src_ref=gsend, dst_ref=gbuf.at[slot], send_sem=g_send.at[k], recv_sem=g_recv.at[slot],
             device_id={"page": target}, device_id_type=pl.DeviceIdType.MESH)
 
-    def g_start(k, carry):
-        g_copy(k, peer_of(k), me).start()
-        return carry
-
-    lax.fori_loop(1, n, g_start, 0)
+    far_first(n, lambda peer: g_copy(peer, peer, me).start())
 
     small[1].wait()
     blank = jnp.zeros((rows, width), BF16)
@@ -122,7 +126,6 @@
     first = me * per_owner
     lanes = lax.broadcasted_iota(jnp.int32, (drafts, 2 * rows), 1)
     keys_at = lax.broadcasted_iota(jnp.int32, (drafts, 2 * rows), 0)
-    fresh = []
     small[2].wait()
     small[3].wait()
     for j in range(pairs):
@@ -132,25 +135,23 @@
         ok = (keys_at <= lanes % drafts) & (head_of >= first) & (head_of < first + per_owner)
         high = jnp.ceil(jnp.max(jnp.where(ok, scores * rate, LOW), axis=0, keepdims=True))
         raised = jnp.where(ok, jnp.exp2(scores * rate - high), 0.0).astype(BF16).astype(F32)
-        fresh.append((high, jnp.sum(raised, axis=0, keepdims=True), raised))
-
-    def g_wait(k, carry):
-        copy = g_copy(k, peer_of(k), peer_of(k))
-        copy.wait_recv()
-        copy.wait_send()
-        return carry
-
-    lax.fori_loop(1, n, g_wait, 0)
-
-    named = [jnp.max(gbuf[t * slots:(t + 1) * slots], axis=0) for t in range(n // slots)]
+        fresh_stats[j, 0:1] = high
+        fresh_stats[j, 1:2] = jnp.sum(raised, axis=0, keepdims=True)
+        fresh_weights[j] = raised
+
+    far_first(n, lambda peer: g_copy(peer, peer, peer).wait_recv())
+
     page_ids = lax.broadcasted_iota(jnp.int32, (pages, LANES), 0) + me * pages
-    picked = []
-    for h in range(kv_heads):
-        hit = named[0][h:h + 1] == page_ids
-        for other in named[1:]:
-            hit = hit | (other[h:h + 1] == page_ids)
-        picked.append(jnp.max(jnp.where(hit, 1.0, 0.0), axis=1, keepdims=True))
-    pair_lanes = lax.broadcasted_iota(jnp.int32, (pages, 2 * rows), 1)
+    hit = gbuf[0] == page_ids
+    for source in range(1, n):
+        hit = hit | (gbuf[source] == page_ids)
+    lane = lax.broadcasted_iota(jnp.int32, (LANES, kv_heads * rows), 0)
+    column = lax.broadcasted_iota(jnp.int32, (LANES, kv_heads * rows), 1)
+    spread = jnp.where(lane // per == column // rows, 1.0, 0.0).astype(BF16)
+    named = dot(jnp.where(hit, 1.0, 0.0).astype(BF16), spread, ((1,), (0,)))
+    for j in range(pairs):
+        picked[j] = named[:, j * 2 * rows:(j + 1) * 2 * rows]
+        loads[j][1].wait()
 
     def o_copy(k, target, slot, owner):
         return pltpu.make_async_remote_copy(
@@ -165,18 +166,23 @@
             device_id={"page": target}, device_id_type=pl.DeviceIdType.MESH)
 
     wide = 8
-    for j in range(pairs):
-        in_use = jnp.where(pair_lanes < rows, picked[2 * j], picked[2 * j + 1]) > 0.5
-        high_fresh, sums_fresh, raised_fresh = fresh[j]
+    plane = me * pairs // n
+    for turn in range(pairs):
+        back = pairs - 1 - turn
+        down = back - jnp.where(back <= plane, 1, 0)
+        up = turn + jnp.where(turn >= plane, 1, 0)
+        j = jnp.where(me * 2 < n, down, up) if back else plane
+        in_use = picked[j] > 0.5
+        high_fresh = fresh_stats[j, 0:1]
+        sums_fresh = fresh_stats[j, 1:2]
         highs = page_high[j]
         top = jnp.maximum(jnp.max(jnp.where(in_use, highs, LOW), axis=0, keepdims=True), high_fresh)
         share = jnp.where(in_use, jnp.exp2(highs - top), 0.0).astype(BF16)
         share_fresh = jnp.exp2(high_fresh - top)
         total = jnp.sum(share.astype(F32) * page_sums[j], axis=0, keepdims=True)
         total = total + share_fresh * sums_fresh
-        loads[j][1].wait()
-        acc = dot((raised_fresh * share_fresh).astype(BF16),
-                  new_values[:, j * 2 * width:(j + 1) * 2 * width], ((0,), (0,)))
+        acc = dot((fresh_weights[j] * share_fresh).astype(BF16),
+                  new_values[:, pl.ds(pl.multiple_of(j * 2 * width, 2 * width), 2 * width)], ((0,), (0,)))
         for p in range(0, pages, wide):
             scaled = weights[j, p:p + wide] * share[p:p + wide][:, None, :]
             acc = acc + dot(scaled.reshape(wide * tokens, 2 * rows),
@@ -185,10 +191,12 @@
         sbuf[j, 1:2] = total
         for a in range(2):
             part = acc[a * rows:(a + 1) * rows, a * width:(a + 1) * width].astype(BF16)
-            obuf[(2 * j + a) * groups:(2 * j + a + 1) * groups] = part.reshape(groups, drafts, width)
+            obuf[pl.ds((2 * j + a) * groups, groups)] = part.reshape(groups, drafts, width)
 
         owned = per_pair // per_owner
-        for o in range(j * owned, (j + 1) * owned):
+        for i in range(owned):
+            o = j * owned + i
+
             @pl.when(me != o)
             def _():
                 s_copy(o, o, me, o).start()
@@ -232,11 +240,7 @@
         for i in range(per_owner):
             fin[:, i * width:(i + 1) * width] = done[i * drafts:(i + 1) * drafts]
 
-        def f_start(k, carry):
-            f_copy(k, peer_of(k), me).start()
-            return carry
-
-        lax.fori_loop(1, n, f_start, 0)
+        far_first(n, lambda peer: f_copy(peer, peer, me).start())
         block_of(me)[...] = fin[...]
 
     if everyone:
@@ -260,12 +264,10 @@
         return carry
 
     lax.fori_loop(0, owners, f_wait, 0)
+    far_first(n, lambda peer: g_copy(peer, peer, peer).wait_send())
+
     def f_sent():
-        def body(k, carry):
-            f_copy(k, peer_of(k), me).wait_send()
-            return carry
-
-        lax.fori_loop(1, n, body, 0)
+        far_first(n, lambda peer: f_copy(peer, peer, me).wait_send())
 
     if everyone:
         f_sent()
@@ -304,8 +306,11 @@
             pltpu.VMEM((pairs, pages, tokens, 2 * rows), BF16),
             pltpu.VMEM((pairs, pages, 2 * rows), F32),
             pltpu.VMEM((pairs, pages, 2 * rows), F32),
-            pltpu.VMEM((n, kv_heads, LANES), jnp.int32),
-            pltpu.VMEM((kv_heads, LANES), jnp.int32),
+            pltpu.VMEM((n, 1, LANES), jnp.int32),
+            pltpu.VMEM((1, LANES), jnp.int32),
+            pltpu.VMEM((pairs, pages, 2 * rows), F32),
+            pltpu.VMEM((pairs, 2, 2 * rows), F32),
+            pltpu.VMEM((pairs, drafts, 2 * rows), F32),
             pltpu.VMEM((heads, drafts, width), BF16),
             pltpu.VMEM((pairs, 2, 2 * rows), F32),
             pltpu.VMEM((n, per_owner, drafts, width), BF16),

time: 24 us -> 22.7 us (0.946)
  Pallas kernels: 23.2 us -> 21.8 us
    pallas_call x1, Pallas kernels: 23.2 us -> 21.8 us  [on_device(): pl.pallas_call(functools.partial(kernel, n, owners, kv_heads, groups), ou...]
where the time goes in v4:
time: 22.7 us; the launch traced here: 22.5 us
  Pallas kernels  21.8 us (96%)
  local copies, waits for them, and re-layouts  0.66 us (3%)
    pallas_call x1, Pallas kernels, on_device(): pl.pallas_call(functools.partial(kernel, n, owners, kv_heads, groups), ou...  21.8 us
    unnamed x1, local copies, waits for them, and re-layouts  0.66 us

profile of v4, /device:TPU:0, one launch (start us, length us, event | category | flops | bytes accessed | tf_op | source)
XLA Modules:
  0.0 22.5 jit_solution(8417840660746995735)
XLA Ops:
  0.0 21.8 %paged_attention.1 = bf16[16,4096]{1,0:T(8,128)(2,1)S(1)} custom-call(bf16[16,4096]{1,0:T(8,128)(2,1)} %queries_hbm.1, bf16[32,64,1024]{2,1,0:T(8,128)(2,1)} %key_hbm.1, bf16[32,64,1024]{2,1,0:T(8,128)(2,1)} %value_hbm.1, bf16[16,1024]{1,0:T(8,128)(2,1)} %new_keys_hbm.1, bf16[16,1024]{1,0:T(8,128)(2,1)} %new_values_hbm.1, s32[8,16]{1,0:T(8,128)} %chosen_hbm.1), custom_call_target="tpu_custom_call" | custom-call | tf_op jit(solution)/shard_map/paged_attention/pallas_call | solution.py:293
  21.9 0.7 %copy.8 = bf16[16,4096]{1,0:T(8,128)(2,1)} copy(bf16[16,4096]{1,0:T(8,128)(2,1)S(1)} %paged_attention.1) | data formatting | bytes 262144

commit v5 on v4

--- a/solution.py
+++ b/solution.py
@@ -46,7 +46,7 @@
             pl.when(peer != me)(lambda: act(peer))
             return carry
 
-        lax.fori_loop(0, count, body, 0)
+        lax.fori_loop(0, count, body, 0, unroll=n <= 16)
 
     barrier = pltpu.get_barrier_semaphore()
 
@@ -55,7 +55,7 @@
                             device_id_type=pl.DeviceIdType.MESH)
         return carry
 
-    lax.fori_loop(1, n, greet, 0)
+    lax.fori_loop(1, n, greet, 0, unroll=n <= 16)
 
     small = [
         pltpu.make_async_copy(src, dst, small_sem.at[i])
@@ -219,7 +219,7 @@
             s_copy(peer_of(k), peer_of(k), peer_of(k), me).wait_recv()
             return carry
 
-        lax.fori_loop(1, n, s_wait, 0)
+        lax.fori_loop(1, n, s_wait, 0, unroll=n <= 16)
         highs = srecv[:, 0, :]
         top = jnp.max(highs, axis=0, keepdims=True)
         share = jnp.exp2(highs - top)
@@ -232,7 +232,7 @@
             o_copy(peer_of(k), peer_of(k), peer_of(k), me).wait_recv()
             return carry
 
-        lax.fori_loop(1, n, o_wait, 0)
+        lax.fori_loop(1, n, o_wait, 0, unroll=n <= 16)
         acc = jnp.zeros((own_rows, width), F32)
         for i in range(n):
             acc = acc + own[:, i:i + 1] * orecv[i].reshape(own_rows, width).astype(F32)
@@ -255,7 +255,7 @@
             o_copy(o, o, me, o).wait_send()
         return carry
 
-    lax.fori_loop(0, owners, sent, 0)
+    lax.fori_loop(0, owners, sent, 0, unroll=n <= 16)
 
     def f_wait(o, carry):
         @pl.when(me != o)
@@ -263,7 +263,7 @@
             f_copy(o, o, o).wait_recv()
         return carry
 
-    lax.fori_loop(0, owners, f_wait, 0)
+    lax.fori_loop(0, owners, f_wait, 0, unroll=n <= 16)
     far_first(n, lambda peer: g_copy(peer, peer, peer).wait_send())
 
     def f_sent():

time: 22.7 us -> 22.2 us (0.978)
  Pallas kernels: 21.8 us -> 21.4 us
    pallas_call x1, Pallas kernels: 21.8 us -> 21.4 us  [on_device(): pl.pallas_call(functools.partial(kernel, n, owners, kv_heads, groups), ou...]
where the time goes in v5:
time: 22.2 us; the launch traced here: 22.1 us
  Pallas kernels  21.4 us (96%)
  local copies, waits for them, and re-layouts  0.66 us (3%)
    pallas_call x1, Pallas kernels, on_device(): pl.pallas_call(functools.partial(kernel, n, owners, kv_heads, groups), ou...  21.4 us
    unnamed x1, local copies, waits for them, and re-layouts  0.66 us

profile of v5, /device:TPU:0, one launch (start us, length us, event | category | flops | bytes accessed | tf_op | source)
XLA Modules:
  0.0 22.1 jit_solution(2119390078002193058)
XLA Ops:
  0.0 21.4 %paged_attention.1 = bf16[16,4096]{1,0:T(8,128)(2,1)S(1)} custom-call(bf16[16,4096]{1,0:T(8,128)(2,1)} %queries_hbm.1, bf16[32,64,1024]{2,1,0:T(8,128)(2,1)} %key_hbm.1, bf16[32,64,1024]{2,1,0:T(8,128)(2,1)} %value_hbm.1, bf16[16,1024]{1,0:T(8,128)(2,1)} %new_keys_hbm.1, bf16[16,1024]{1,0:T(8,128)(2,1)} %new_values_hbm.1, s32[8,16]{1,0:T(8,128)} %chosen_hbm.1), custom_call_target="tpu_custom_call" | custom-call | tf_op jit(solution)/shard_map/paged_attention/pallas_call | solution.py:293
  21.4 0.7 %copy.8 = bf16[16,4096]{1,0:T(8,128)(2,1)} copy(bf16[16,4096]{1,0:T(8,128)(2,1)S(1)} %paged_attention.1) | data formatting | bytes 262144
